TPU v7x, 32 devices: a whole 2x2x4 slice. The times are simulated.
32 devices in a mesh: dp: 16 (over z, x, core), ens: 2 (over y).
Axes of the slice: x: 2, y: 2, z: 4, core: 2. Of those that a mesh axis runs over, the one named last changes fastest.
Arguments:
- embeddings: bfloat16 [12288, 1024], P('dp'), may hold values from -6 to 6
- valid_mask: int32 [12288], P('dp'), may hold values 0 or 1
- first_weight: bfloat16 [2, 1024, 4096], P(None, 'dp', 'ens'), may hold values from -0.1875 to 0.1875
- second_weight: bfloat16 [2, 4096, 128], P(None, 'ens'), may hold values from -0.09375 to 0.09375
- thresholds: int32 [2], replicated, may hold values from -256 to 256
Outputs:
- mean_logits: float32 [12288, 128], P('dp')
- kept_share: float32 [2], P('ens')
- agree_share: float32 [2], P('ens')
All inputs are finite; a program needn't handle non-finite values. No bound on the sum of `valid_mask` on one device may be relied on, other than what follows from the above.
Results may differ from a plain program's by a relative error of at most 0.0044.
Values may be sent and summed in bfloat16 or wider, within the bound.
A program may use at most 64 MiB of HBM per device.

v0:
```python
import functools

import jax
import jax.numpy as jnp
from jax import lax
from jax.experimental import pallas as pl
from jax.experimental.pallas import tpu as pltpu
from jax.sharding import PartitionSpec as P

MESH = pl.DeviceIdType.MESH
COLS = 512
LAG = 2
PARTS = 2
SLOTS = 2


def geometry(mesh):
    line = [tuple(d.coords) for d in mesh.devices.reshape(mesh.devices.shape[0], -1)[:, 0]]
    cores = sum(c == line[0] for c in line)
    chips = line[::cores]
    inner = 1
    if len(chips) > 1:
        axis = [a != b for a, b in zip(chips[0], chips[1])].index(True)
        while inner < len(chips) and chips[inner][axis] == chips[0][axis] + inner:
            inner += 1
    return len(chips) // inner, inner, cores


def turned_period(nz, nx):
    even = (nz - 1) * nx - (nx - 1)
    slope = (nz - 1) * (nx - 1) + (nz - 1) * (nx - 1)
    share = 1.0 - even / slope if slope else 0.0
    return round(1 / share) if share > 0 else 0


def kernel(
    geo, n_ens, emb_hbm, mask_ref, fw_hbm, sw_hbm, thr_ref, out_ref, kept_ref, agree_ref,
    w, emb, sw, acc, part, sc, tot,
    local_sem, emb_sem, send_sem, recv_sem, part_send, part_recv, sc_send, sc_recv, tot_sem, core_send, core_recv,
):
    nz, nx, nc = geo
    n_dp = nz * nx * nc
    n_chips = nz * nx
    members, rows, units = fw_hbm.shape
    per_member = units // COLS
    chunks = members * per_member
    docs, classes = out_ref.shape
    period = turned_period(nz, nx)
    reach = nz - 1 + nx - 1
    slots = send_sem.shape[0]

    me = lax.axis_index("dp")
    ens = lax.axis_index("ens")
    core = lax.rem(me, nc)
    chip = me // nc
    z, x = chip // nx, lax.rem(chip, nx)

    def origin_rows(origin):
        return pl.ds(pl.multiple_of(origin * rows, rows), rows)

    def own_copy(c):
        cols = pl.ds(pl.multiple_of(lax.rem(c, per_member) * COLS, COLS), COLS)
        return pltpu.make_async_copy(
            fw_hbm.at[c // per_member, :, cols], w.at[c, origin_rows(me), :], local_sem.at[c]
        )

    for c in range(chunks):
        own_copy(jnp.int32(c)).start()
    emb_copy = pltpu.make_async_copy(emb_hbm, emb, emb_sem.at[0])
    sw_copy = pltpu.make_async_copy(sw_hbm, sw, emb_sem.at[1])
    emb_copy.start()
    sw_copy.start()

    barrier = pltpu.get_barrier_semaphore()
    dirs = []
    if nz > 1:
        dirs += [("z", 1), ("z", -1)]
    if nx > 1:
        dirs += [("x", 1), ("x", -1)]
    dirs += [("c", k) for k in range(1, nc)]

    def target(d):
        kind, k = d
        if kind == "z":
            return me + k * nx * nc
        if kind == "x":
            return me + k * nc
        return chip * nc + lax.rem(core + k, nc)

    def there(d):
        kind, k = d
        if kind == "c":
            return None
        at, n = (z, nz) if kind == "z" else (x, nx)
        return at + 1 < n if k > 0 else at > 0

    waits = jnp.int32(nc - 1 + n_ens - 1)
    for d in dirs:
        ok = there(d)
        if ok is None:
            pl.semaphore_signal(barrier, inc=1, device_id={"dp": target(d)}, device_id_type=MESH)
        else:
            @pl.when(ok)
            def _():
                pl.semaphore_signal(barrier, inc=1, device_id={"dp": target(d)}, device_id_type=MESH)
            waits = waits + ok.astype(jnp.int32)
    for k in range(1, n_ens):
        pl.semaphore_signal(
            barrier, inc=1, device_id={"ens": lax.rem(ens + k, n_ens)}, device_id_type=MESH
        )
    pl.semaphore_wait(barrier, waits)

    def turned(c):
        if not period:
            return jnp.bool_(False)
        return lax.rem(c * nc + core, period) == period // 2

    def goes(d, c, zo, xo):
        kind, k = d
        if kind == "c":
            return c >= 0
        inner_first = turned(c)
        if kind == "z":
            away = (z >= zo) if k > 0 else (z <= zo)
            return away & there(d) & ((xo == x) | inner_first)
        away = (x >= xo) if k > 0 else (x <= xo)
        return away & there(d) & ((zo == z) | jnp.logical_not(inner_first))

    def sending(i, d, c, zo, xo):
        place = zo * nx + xo
        origin = place * nc + core
        block = w.at[c, origin_rows(origin), :]
        if d[0] == "c":
            sems = core_send.at[c, d[1]], core_recv.at[c, d[1]]
        else:
            sems = send_sem.at[lax.rem(c, slots), i, place], recv_sem.at[c, place]
        return pltpu.make_async_remote_copy(
            src_ref=block, dst_ref=block, send_sem=sems[0], recv_sem=sems[1],
            device_id={"dp": target(d)}, device_id_type=MESH,
        )

    def from_cores(c, k):
        blocks = w.at[c, pl.ds(0, n_chips * rows), :]
        return pltpu.make_async_remote_copy(
            src_ref=blocks, dst_ref=blocks,
            send_sem=core_send.at[c, k], recv_sem=core_recv.at[c, k],
            device_id={"dp": target(("c", k))}, device_id_type=MESH,
        )

    def arrived(c, place):
        block = w.at[c, origin_rows(place * nc + core), :]
        pltpu.make_async_remote_copy(
            src_ref=block, dst_ref=block, send_sem=send_sem.at[0, 0, 0], recv_sem=recv_sem.at[c, place],
            device_id={"dp": target(dirs[-1])}, device_id_type=MESH,
        ).wait_recv()

    def place_of(k):
        kz, kx = divmod(k, nx)
        return lax.rem(z + kz, nz), lax.rem(x + kx, nx)

    acc[...] = jnp.zeros_like(acc)

    def compute(done):
        @pl.when(done >= 0)
        def _():
            @pl.when(done == 0)
            def _():
                emb_copy.wait()
                sw_copy.wait()
            for o in range(1, nc):
                from_cores(done, o).wait_recv()
            m = done // per_member
            cols = pl.ds(pl.multiple_of(lax.rem(done, per_member) * COLS, COLS), COLS)
            hidden = jnp.maximum(
                jnp.dot(emb[...], w[done], preferred_element_type=jnp.float32), 0.0
            ).astype(jnp.bfloat16)
            acc[m] += jnp.dot(hidden, sw[m, cols, :], preferred_element_type=jnp.float32)

    def step(t, carry):
        for k in range(n_chips):
            zo, xo = place_of(k)
            c = t - LAG * (jnp.abs(z - zo) + jnp.abs(x - xo))

            @pl.when((c >= 0) & (c < chunks))
            def _():
                if k == 0:
                    own_copy(c).wait()
                else:
                    arrived(c, zo * nx + xo)
                for i, d in enumerate(dirs):
                    if d[0] == "c":
                        sending(i, d, c, zo, xo).start()
                        continue

                    @pl.when((c >= slots) & goes(d, c - slots, zo, xo))
                    def _():
                        sending(i, d, c - slots, zo, xo).wait_send()

                    @pl.when(goes(d, c, zo, xo))
                    def _():
                        sending(i, d, c, zo, xo).start()

            if k == n_chips - 1:
                compute(t - LAG * reach - 1)
        return carry

    lax.fori_loop(0, chunks + LAG * reach + 1, step, 0)

    lines = sc.shape[1]
    levels = lax.broadcasted_iota(jnp.int32, (lines, classes), 1).astype(jnp.float32)
    grades = (2.0 * levels / (classes - 1) - 1.0) * jnp.sqrt(jnp.float32(3.0 / classes))
    line = lax.broadcasted_iota(jnp.int32, (lines, classes), 0)
    own_scores = jnp.zeros((lines, docs), jnp.float32)
    for m in range(members):
        own_scores += lax.dot_general(
            jnp.where(line == m, grades, 0.0), acc[m], (((1,), (1,)), ((), ())),
            precision=lax.Precision.HIGHEST, preferred_element_type=jnp.float32,
        )
    sc[ens] = own_scores

    def sc_copy(k):
        return pltpu.make_async_remote_copy(
            src_ref=sc.at[ens], dst_ref=sc.at[ens], send_sem=sc_send.at[k], recv_sem=sc_recv.at[ens],
            device_id={"ens": lax.rem(ens + k, n_ens)}, device_id_type=MESH,
        )

    def part_copy(k, b):
        piece = part.at[ens, pl.ds(b * (docs // PARTS), docs // PARTS), :]
        return pltpu.make_async_remote_copy(
            src_ref=piece, dst_ref=piece, send_sem=part_send.at[k, b], recv_sem=part_recv.at[ens, b],
            device_id={"ens": lax.rem(ens + k, n_ens)}, device_id_type=MESH,
        )

    for k in range(1, n_ens):
        sc_copy(k).start()
    for b in range(PARTS):
        piece = pl.ds(b * (docs // PARTS), docs // PARTS)
        total = acc[0, piece, :]
        for m in range(1, members):
            total += acc[m, piece, :]
        part[ens, piece, :] = (total * (1.0 / members)).astype(jnp.bfloat16)
        for k in range(1, n_ens):
            part_copy(k, b).start()

    for k in range(1, n_ens):
        other = lax.rem(ens + k, n_ens)
        pltpu.make_async_remote_copy(
            src_ref=sc.at[other], dst_ref=sc.at[other], send_sem=sc_send.at[k], recv_sem=sc_recv.at[other],
            device_id={"ens": other}, device_id_type=MESH,
        ).wait_recv()
    scores = sc[0]
    for k in range(1, n_ens):
        scores += sc[k]
    row = lax.broadcasted_iota(jnp.int32, (lines, docs), 0)
    cutoff = jnp.zeros((lines, docs), jnp.float32)
    mean_cutoff = jnp.float32(0.0)
    for m in range(members):
        level = thr_ref[m].astype(jnp.float32) * (1.0 / 256.0)
        cutoff = jnp.where(row == m, level, cutoff)
        mean_cutoff += level * (1.0 / members)
    kept = mask_ref[...].reshape(1, docs).astype(jnp.float32) * jax.nn.sigmoid(4.0 * (scores - cutoff))
    ens_score = jnp.sum(scores, axis=0, keepdims=True) * (1.0 / members)
    ens_kept = jax.nn.sigmoid(4.0 * (ens_score - mean_cutoff))
    kept_sum = jnp.sum(kept, axis=1, keepdims=True)
    agree_sum = jnp.sum(kept * ens_kept, axis=1, keepdims=True)
    lane = lax.broadcasted_iota(jnp.int32, (lines, 128), 1)
    tot[me] = jnp.where(lane == 0, kept_sum, jnp.where(lane == 1, agree_sum, 0.0))

    def tot_copy(k):
        return pltpu.make_async_remote_copy(
            src_ref=tot.at[me], dst_ref=tot.at[me], send_sem=tot_sem.at[0], recv_sem=tot_sem.at[1],
            device_id={"dp": lax.rem(me + k, n_dp)}, device_id_type=MESH,
        )

    tiles = tot.at[pl.ds(0, n_dp - 1)]
    all_tot = pltpu.make_async_remote_copy(
        src_ref=tiles, dst_ref=tiles, send_sem=tot_sem.at[0], recv_sem=tot_sem.at[1],
        device_id={"dp": lax.rem(me + 1, n_dp)}, device_id_type=MESH,
    )

    for k in range(1, n_dp):
        tot_copy(k).start()

    for b in range(PARTS):
        piece = pl.ds(b * (docs // PARTS), docs // PARTS)
        for k in range(1, n_ens):
            other = lax.rem(ens + k, n_ens)
            block = part.at[other, piece, :]
            pltpu.make_async_remote_copy(
                src_ref=block, dst_ref=block, send_sem=part_send.at[k, b], recv_sem=part_recv.at[other, b],
                device_id={"ens": other}, device_id_type=MESH,
            ).wait_recv()
        total = part[0, piece, :].astype(jnp.float32)
        for k in range(1, n_ens):
            total += part[k, piece, :].astype(jnp.float32)
        out_ref[piece, :] = total

    all_tot.wait_recv()
    sums = tot[0]
    for k in range(1, n_dp):
        sums += tot[k]
    sums = sums / docs
    own = members // n_ens
    row = lax.broadcasted_iota(jnp.int32, (lines, 128), 0)
    for j in range(own):
        mine = row == ens * own + j
        kept_ref[j] = jnp.sum(jnp.where(mine & (lane == 0), sums, 0.0))
        agree_ref[j] = jnp.sum(jnp.where(mine & (lane == 1), sums, 0.0))

    for k in range(n_chips):
        zo, xo = place_of(k)
        for c in range(max(0, chunks - slots), chunks):
            for i, d in enumerate(dirs):
                if d[0] != "c":
                    @pl.when(goes(d, jnp.int32(c), zo, xo))
                    def _():
                        sending(i, d, jnp.int32(c), zo, xo).wait_send()
    for c in range(chunks):
        for k in range(1, nc):
            from_cores(c, k).wait_send()
    for k in range(1, n_ens):
        sc_copy(k).wait_send()
        for b in range(PARTS):
            part_copy(k, b).wait_send()
    all_tot.wait_send()


def solution(mesh):
    geo = geometry(mesh)
    nz, nx, nc = geo
    n_dp, n_ens = mesh.shape["dp"], mesh.shape["ens"]

    def on_device(embeddings, valid_mask, first_weight, second_weight, thresholds):
        docs, width = embeddings.shape
        members, rows, units = first_weight.shape
        classes = second_weight.shape[2]
        chunks = members * units // COLS
        own = members // n_ens
        lines = -(-members // 8) * 8
        dma = pltpu.SemaphoreType.DMA
        hbm, vmem, smem = (pl.BlockSpec(memory_space=s) for s in (pl.ANY, pltpu.VMEM, pltpu.SMEM))
        return pl.pallas_call(
            functools.partial(kernel, geo, n_ens),
            out_shape=(
                jax.ShapeDtypeStruct((docs, classes), jnp.float32),
                jax.ShapeDtypeStruct((own,), jnp.float32),
                jax.ShapeDtypeStruct((own,), jnp.float32),
            ),
            in_specs=[hbm, vmem, hbm, hbm, smem],
            out_specs=(vmem, smem, smem),
            scratch_shapes=[
                pltpu.VMEM((chunks, width, COLS), jnp.bfloat16),
                pltpu.VMEM((docs, width), jnp.bfloat16),
                pltpu.VMEM(second_weight.shape, jnp.bfloat16),
                pltpu.VMEM((members, docs, classes), jnp.float32),
                pltpu.VMEM((n_ens, docs, classes), jnp.bfloat16),
                pltpu.VMEM((n_ens, lines, docs), jnp.float32),
                pltpu.VMEM((n_dp, lines, 128), jnp.float32),
                dma((chunks,)),
                dma((2,)),
                dma((SLOTS, 4, nz * nx)),
                dma((chunks, nz * nx)),
                dma((n_ens, PARTS)),
                dma((n_ens, PARTS)),
                dma((n_ens,)),
                dma((n_ens,)),
                dma((2,)),
                dma((chunks, nc)),
                dma((chunks, nc)),
            ],
            compiler_params=pltpu.CompilerParams(
                collective_id=0, has_side_effects=True, vmem_limit_bytes=63 * 1024 * 1024
            ),
        )(embeddings, valid_mask, first_weight, second_weight, thresholds)

    return jax.shard_map(
        on_device,
        mesh=mesh,
        in_specs=(P("dp", None), P("dp"), P(None, "dp", "ens"), P(None, "ens", None), P()),
        out_specs=(P("dp", None), P("ens"), P("ens")),
        check_vma=False,
    )
```

profile of v0, /device:TPU:0, one launch (start us, length us, event | category | flops | bytes accessed | tf_op | source)
XLA Modules:
  0.0 69.6 jit_solution(7199199657719422946)
XLA Ops:
  0.6 63.6 %shard_map.76 = (f32[768,128]{1,0:T(8,128)}, f32[1]{0:T(128)}, f32[1]{0:T(128)}) custom-call(bf16[768,1024]{1,0:T(8,128)(2,1)} %emb_hbm.1, s32[768]{0:T(1024)} %mask_ref.1, bf16[2,64,2048]{2,1,0:T(8,128)(2,1)} %fw_hbm.1, bf16[2,2048,128]{2,1,0:T(8,128)(2,1)} %sw_hbm.1, s32[2]{0:T(128)} %thr_ref.1), custom_call_target="tpu_custom_call" | custom-call | tf_op jit(solution)/shard_map/pallas_call | solution.py:342
  64.3 1.8 %copy.11 = f32[768,128]{1,0:T(8,128)} copy(f32[768,128]{1,0:T(8,128)} %get-tuple-element.6) | data formatting | bytes 786432
where the time goes:
time: 69.8 us; the launch traced here: 69.6 us
  Pallas kernels  63.6 us (91%)
  between operations  4.21 us (6%)
  local copies, waits for them, and re-layouts  1.77 us (3%)
    pallas_call x1, Pallas kernels, on_device(): pl.pallas_call(functools.partial(kernel, geo, n_ens), out_shape=(jax.Shap...  63.6 us
    unnamed x1, local copies, waits for them, and re-layouts  1.77 us

commit v1 on v0

v1 whole, which is shorter than its diff:
```python
import functools
import math

import jax
import jax.numpy as jnp
from jax import lax
from jax.experimental import pallas as pl
from jax.experimental.pallas import tpu as pltpu
from jax.sharding import PartitionSpec as P

MESH = pl.DeviceIdType.MESH
COLS = 256
ROWS = 256
PIECES = 4
PARTS = 4


def geometry(mesh):
    line = [tuple(d.coords) for d in mesh.devices.reshape(mesh.devices.shape[0], -1)[:, 0]]
    cores = sum(c == line[0] for c in line)
    chips = line[::cores]
    inner = 1
    if len(chips) > 1:
        axis = [a != b for a, b in zip(chips[0], chips[1])].index(True)
        while inner < len(chips) and chips[inner][axis] == chips[0][axis] + inner:
            inner += 1
    return len(chips) // inner, inner, cores


def kernel(
    geo, n_ens, emb_hbm, mask_hbm, fw_hbm, sw_hbm, thr_hbm, out_ref, share_ref,
    w, emb, sw, acc, hid, mask, thr, px_out, px_in, part, sc_out, sc_in, tot,
    local_sem, load_sem, z_send, w_recv, x_send, core_send, core_recv, doc_send, doc_recv, fwd_send,
    px_send, px_recv, part_send, part_recv, sc_send, sc_recv, tot_sem,
):
    nz, nx, nc = geo
    n_dp = nz * nx * nc
    n_chips = nz * nx
    members, rows, units = fw_hbm.shape
    chunks, width, cols = w.shape
    per_member = chunks // members
    share = units // nx
    docs, classes = out_ref.shape
    doc_part = docs // n_ens
    doc_piece = doc_part // PIECES
    step_rows = math.gcd(docs, ROWS)

    me = lax.axis_index("dp")
    ens = lax.axis_index("ens")
    core = lax.rem(me, nc)
    chip = me // nc
    z, x = chip // nx, lax.rem(chip, nx)

    def device(zz, xx, cc):
        return (zz * nx + xx) * nc + cc

    def turn(at, k, n):
        return lax.rem(at + k, n)

    def slot(xx):
        return pl.ds(pl.multiple_of(xx * docs, docs), docs)

    def origin_rows(origin):
        return pl.ds(pl.multiple_of(origin * rows, rows), rows)

    def share_cols(xx, c):
        return pl.ds(pl.multiple_of(xx * share + lax.rem(c, per_member) * cols, cols), cols)

    def own_copy(c):
        return pltpu.make_async_copy(
            fw_hbm.at[c // per_member, :, share_cols(x, c)], w.at[c, origin_rows(me), :], local_sem.at[c]
        )

    def loop(n, body):
        def step(i, carry):
            body(i)
            return carry
        lax.fori_loop(0, n, step, 0)

    loop(chunks, lambda c: own_copy(c).start())
    emb_copy = pltpu.make_async_copy(emb_hbm, emb.at[slot(x), :], load_sem.at[0])
    sw_copy = pltpu.make_async_copy(
        sw_hbm.at[:, pl.ds(pl.multiple_of(x * share, share), share), :], sw, load_sem.at[1]
    )
    mask_copy = pltpu.make_async_copy(mask_hbm, mask, load_sem.at[2])
    thr_copy = pltpu.make_async_copy(thr_hbm, thr, load_sem.at[3])

    barrier = pltpu.get_barrier_semaphore()
    waits = jnp.int32(nc - 1 + nx * n_ens - 1)
    for s in (1, -1):
        if nz > 1:
            ok = (z + s >= 0) & (z + s < nz)

            @pl.when(ok)
            def _():
                pl.semaphore_signal(barrier, inc=1, device_id={"dp": me + s * nx * nc}, device_id_type=MESH)
            waits = waits + ok.astype(jnp.int32)
    for k in range(1, nc):
        pl.semaphore_signal(
            barrier, inc=1, device_id={"dp": device(z, x, turn(core, k, nc))}, device_id_type=MESH
        )
    others = [(k, e) for k in range(nx) for e in range(n_ens) if k or e]
    for k, e in others:
        pl.semaphore_signal(
            barrier, inc=1,
            device_id={"dp": device(z, turn(x, k, nx), core), "ens": turn(ens, e, n_ens)}, device_id_type=MESH,
        )
    pl.semaphore_wait(barrier, waits)

    def block(c, zo, xo):
        return w.at[c, origin_rows(device(zo, xo, core)), :]

    def x_weights(k, c):
        xp = turn(x, k, nx)
        return pltpu.make_async_remote_copy(
            src_ref=fw_hbm.at[c // per_member, :, share_cols(xp, c)], dst_ref=w.at[c, origin_rows(me), :],
            send_sem=x_send.at[k], recv_sem=w_recv.at[z * nx + x, c],
            device_id={"dp": device(z, xp, core)}, device_id_type=MESH,
        )

    def doc_rows(xx, e, i):
        return pl.ds(pl.multiple_of(xx * docs + e * doc_part + i * doc_piece, doc_piece), doc_piece)

    def x_docs(k, i):
        xp = turn(x, k, nx)
        return pltpu.make_async_remote_copy(
            src_ref=emb_hbm.at[doc_rows(0, ens, i), :], dst_ref=emb.at[doc_rows(x, ens, i), :],
            send_sem=doc_send.at[k], recv_sem=doc_recv.at[x, ens, i],
            device_id={"dp": device(z, xp, core)}, device_id_type=MESH,
        )

    def doc_forward(k, i, e):
        xp = turn(x, k, nx)
        piece = emb.at[doc_rows(xp, ens, i), :]
        return pltpu.make_async_remote_copy(
            src_ref=piece, dst_ref=piece, send_sem=fwd_send.at[k, e], recv_sem=doc_recv.at[xp, ens, i],
            device_id={"ens": turn(ens, e, n_ens)}, device_id_type=MESH,
        )

    def doc_arrived(k, i, e):
        xp = turn(x, k, nx)
        ep = turn(ens, e, n_ens)
        piece = emb.at[doc_rows(xp, ep, i), :]
        pltpu.make_async_remote_copy(
            src_ref=piece, dst_ref=piece, send_sem=fwd_send.at[k, 0], recv_sem=doc_recv.at[xp, ep, i],
            device_id={"dp": me}, device_id_type=MESH,
        ).wait_recv()

    def z_copy(c, zo, xo, s):
        place = zo * nx + xo
        return pltpu.make_async_remote_copy(
            src_ref=block(c, zo, xo), dst_ref=block(c, zo, xo),
            send_sem=z_send.at[0 if s > 0 else 1, place], recv_sem=w_recv.at[place, c],
            device_id={"dp": me + s * nx * nc}, device_id_type=MESH,
        )

    def core_copy(c, zo, xo, k):
        return pltpu.make_async_remote_copy(
            src_ref=block(c, zo, xo), dst_ref=block(c, zo, xo),
            send_sem=core_send.at[k], recv_sem=core_recv.at[c, k],
            device_id={"dp": device(z, x, turn(core, k, nc))}, device_id_type=MESH,
        )

    def pass_on(c, zo, xo, sides):
        for s in sides:
            @pl.when((z + s >= 0) & (z + s < nz))
            def _():
                z_copy(c, zo, xo, s).start()
        for k in range(1, nc):
            core_copy(c, zo, xo, k).start()

    def arrived(c, zo, xo):
        pltpu.make_async_remote_copy(
            src_ref=block(c, zo, xo), dst_ref=block(c, zo, xo),
            send_sem=z_send.at[0, 0], recv_sem=w_recv.at[zo * nx + xo, c],
            device_id={"dp": me}, device_id_type=MESH,
        ).wait_recv()

    def from_cores(c, k):
        blocks = w.at[c, pl.ds(0, n_chips * rows), :]
        return pltpu.make_async_remote_copy(
            src_ref=blocks, dst_ref=blocks, send_sem=core_send.at[k], recv_sem=core_recv.at[c, k],
            device_id={"dp": device(z, x, turn(core, k, nc))}, device_id_type=MESH,
        )

    for k in range(1, nx):
        loop(chunks, lambda c: x_weights(k, c).start())
        for i in range(PIECES):
            x_docs(k, i).start()

    def first(c):
        own_copy(c).wait()
        pass_on(c, z, x, (1, -1))
    loop(chunks, first)
    for copy in (emb_copy, sw_copy, mask_copy, thr_copy):
        copy.start()
    acc[...] = jnp.zeros_like(acc)

    for k in range(1, nx):
        def second(c):
            arrived(c, z, turn(x, k, nx))
            pass_on(c, z, turn(x, k, nx), (1, -1))
        loop(chunks, second)

    def take(d, c):
        for s in (1, -1):
            zo = z + s * d

            @pl.when((zo >= 0) & (zo < nz))
            def _():
                for k in range(nx):
                    arrived(c, zo, turn(x, k, nx))
                    pass_on(c, zo, turn(x, k, nx), (-s,))

    def forward_docs(i):
        for k in range(1, nx):
            doc_arrived(k, i, 0)
            for e in range(1, n_ens):
                doc_forward(k, i, e).start()

    sent = 0
    for d in range(1, nz - 1):
        due = {chunks - 1: [0]} if d == 1 else {}
        if d == 2:
            for i in range(1, PIECES):
                due.setdefault((i * chunks) // (PIECES - 1) - 1, []).append(i)

        def relay(c):
            take(d, c)
            for at, pieces in due.items():
                @pl.when(c == at)
                def _():
                    for i in pieces:
                        forward_docs(i)
        loop(chunks, relay)
        sent += sum(len(v) for v in due.values())
    for i in range(sent, PIECES):
        forward_docs(i)
    for k in range(1, nx):
        for e in range(1, n_ens):
            for i in range(PIECES):
                doc_arrived(k, i, e)
    for copy in (emb_copy, sw_copy, mask_copy, thr_copy):
        copy.wait()

    def compute(c):
        for k in range(1, nc):
            from_cores(c, k).wait_recv()
        m = c // per_member
        at = pl.ds(pl.multiple_of(lax.rem(c, per_member) * cols, cols), cols)
        for r in range(0, nx * docs, step_rows):
            hid[pl.ds(r, step_rows), :] = jnp.maximum(
                jnp.dot(emb[pl.ds(r, step_rows), :], w[c], preferred_element_type=jnp.float32), 0.0
            ).astype(jnp.bfloat16)
        acc[m] += jnp.dot(hid[...], sw[m, at, :], preferred_element_type=jnp.float32)

    def last(c):
        if nz > 1:
            @pl.when(c < chunks)
            def _():
                take(nz - 1, c)

        @pl.when(c > 0)
        def _():
            compute(c - 1)
    loop(chunks + 1, last)

    lines = sc_in.shape[1]
    wide = members * classes
    lane = lax.broadcasted_iota(jnp.int32, (lines, wide), 1)
    line = lax.broadcasted_iota(jnp.int32, (lines, wide), 0)
    levels = lax.rem(lane, classes).astype(jnp.float32)
    grades = (2.0 * levels / (classes - 1) - 1.0) * jnp.sqrt(jnp.float32(3.0 / classes))
    grades = jnp.where(line == lane // classes, grades, 0.0)
    g_hi = grades.astype(jnp.bfloat16)
    g_lo = (grades - g_hi.astype(jnp.float32)).astype(jnp.bfloat16)
    g = jnp.concatenate([g_hi, g_lo], axis=0)

    def scores_of(xx):
        both = jnp.concatenate([acc[m, slot(xx), :] for m in range(members)], axis=1)
        hi = both.astype(jnp.bfloat16)
        lo = (both - hi.astype(jnp.float32)).astype(jnp.bfloat16)
        dims = (((1,), (1,)), ((), ()))
        s = lax.dot_general(g, hi, dims, preferred_element_type=jnp.float32)
        s += lax.dot_general(g, lo, dims, preferred_element_type=jnp.float32)
        return s[:lines] + s[lines:]

    mine = x * n_ens + ens

    def sc_copy(k, e):
        xp, ep = turn(x, k, nx), turn(ens, e, n_ens)
        return pltpu.make_async_remote_copy(
            src_ref=sc_out.at[k], dst_ref=sc_in.at[mine],
            send_sem=sc_send.at[k, e], recv_sem=sc_recv.at[mine],
            device_id={"dp": device(z, xp, core), "ens": ep}, device_id_type=MESH,
        )

    def sc_arrived(k, e):
        src = turn(x, k, nx) * n_ens + turn(ens, e, n_ens)
        pltpu.make_async_remote_copy(
            src_ref=sc_out.at[k], dst_ref=sc_in.at[src],
            send_sem=sc_send.at[k, e], recv_sem=sc_recv.at[src],
            device_id={"dp": me}, device_id_type=MESH,
        ).wait_recv()

    for k in list(range(1, nx)) + [0]:
        xp = turn(x, k, nx)
        s = scores_of(xp)
        sc_out[k] = s
        if k == 0:
            sc_in[mine] = s
        for e in range(n_ens):
            if k or e:
                sc_copy(k, e).start()

    def piece_of(b):
        return pl.ds(b * (docs // PARTS), docs // PARTS)

    def mean_part(xp, b):
        rows_b = pl.ds(pl.multiple_of(xp * docs + b * (docs // PARTS), docs // PARTS), docs // PARTS)
        total = acc[0, rows_b, :]
        for m in range(1, members):
            total += acc[m, rows_b, :]
        return total * (1.0 / members)

    def px_copy(k, b):
        return pltpu.make_async_remote_copy(
            src_ref=px_out.at[k, piece_of(b), :], dst_ref=px_in.at[x, piece_of(b), :],
            send_sem=px_send.at[k, b], recv_sem=px_recv.at[x, b],
            device_id={"dp": device(z, turn(x, k, nx), core)}, device_id_type=MESH,
        )

    def px_arrived(k, b):
        xp = turn(x, k, nx)
        pltpu.make_async_remote_copy(
            src_ref=px_in.at[xp, piece_of(b), :], dst_ref=px_in.at[xp, piece_of(b), :],
            send_sem=px_send.at[k, b], recv_sem=px_recv.at[xp, b],
            device_id={"dp": me}, device_id_type=MESH,
        ).wait_recv()

    def part_copy(e, b):
        piece = part.at[ens, piece_of(b), :]
        return pltpu.make_async_remote_copy(
            src_ref=piece, dst_ref=piece, send_sem=part_send.at[e, b], recv_sem=part_recv.at[ens, b],
            device_id={"ens": turn(ens, e, n_ens)}, device_id_type=MESH,
        )

    for b in range(PARTS):
        for k in range(1, nx):
            px_out[k, piece_of(b), :] = mean_part(turn(x, k, nx), b).astype(jnp.bfloat16)
            px_copy(k, b).start()

    def relay_part(b):
        total = mean_part(x, b)
        for k in range(1, nx):
            px_arrived(k, b)
            total += px_in[turn(x, k, nx), piece_of(b), :].astype(jnp.float32)
        part[ens, piece_of(b), :] = total.astype(jnp.bfloat16)
        for e in range(1, n_ens):
            part_copy(e, b).start()

    relay_part(0)
    for k, e in others:
        sc_arrived(k, e)
    scores = sc_in[0]
    for k in range(1, nx * n_ens):
        scores += sc_in[k]
    row = lax.broadcasted_iota(jnp.int32, (lines, docs), 0)
    cutoff = jnp.zeros((lines, docs), jnp.float32)
    mean_cutoff = jnp.float32(0.0)
    for m in range(members):
        level = thr[m].astype(jnp.float32) * (1.0 / 256.0)
        cutoff = jnp.where(row == m, level, cutoff)
        mean_cutoff += level * (1.0 / members)
    kept = mask[...].reshape(1, docs).astype(jnp.float32) * jax.nn.sigmoid(4.0 * (scores - cutoff))
    ens_score = jnp.sum(scores, axis=0, keepdims=True) * (1.0 / members)
    ens_kept = jax.nn.sigmoid(4.0 * (ens_score - mean_cutoff))
    kept_sum = jnp.sum(kept, axis=1, keepdims=True)
    agree_sum = jnp.sum(kept * ens_kept, axis=1, keepdims=True)
    lane = lax.broadcasted_iota(jnp.int32, (lines, 128), 1)
    tot[me] = jnp.where(lane == 0, kept_sum, jnp.where(lane == 1, agree_sum, 0.0))

    def tot_copy(k):
        return pltpu.make_async_remote_copy(
            src_ref=tot.at[me], dst_ref=tot.at[me], send_sem=tot_sem.at[0], recv_sem=tot_sem.at[1],
            device_id={"dp": lax.rem(me + k, n_dp)}, device_id_type=MESH,
        )

    tiles = tot.at[pl.ds(0, n_dp - 1)]
    all_tot = pltpu.make_async_remote_copy(
        src_ref=tiles, dst_ref=tiles, send_sem=tot_sem.at[0], recv_sem=tot_sem.at[1],
        device_id={"dp": lax.rem(me + 1, n_dp)}, device_id_type=MESH,
    )
    for k in range(1, n_dp):
        tot_copy(k).start()

    for b in range(1, PARTS):
        relay_part(b)

    for b in range(PARTS):
        for e in range(1, n_ens):
            other = turn(ens, e, n_ens)
            block_in = part.at[other, piece_of(b), :]
            pltpu.make_async_remote_copy(
                src_ref=block_in, dst_ref=block_in, send_sem=part_send.at[e, b], recv_sem=part_recv.at[other, b],
                device_id={"ens": other}, device_id_type=MESH,
            ).wait_recv()
        total = part[0, piece_of(b), :].astype(jnp.float32)
        for e in range(1, n_ens):
            total += part[e, piece_of(b), :].astype(jnp.float32)
        out_ref[piece_of(b), :] = total

    all_tot.wait_recv()
    sums = tot[0]
    for k in range(1, n_dp):
        sums += tot[k]
    sums = sums / docs
    own = members // n_ens
    row = lax.broadcasted_iota(jnp.int32, (lines, 128), 0)
    for j in range(own):
        hit = row == ens * own + j
        for i in range(2):
            share_ref[i * own + j] = jnp.sum(jnp.where(hit & (lane == i), sums, 0.0))

    for k in range(1, nx):
        whole = w.at[:, origin_rows(me), :]
        pltpu.make_async_remote_copy(
            src_ref=whole, dst_ref=whole, send_sem=x_send.at[k], recv_sem=w_recv.at[0, 0],
            device_id={"dp": device(z, turn(x, k, nx), core)}, device_id_type=MESH,
        ).wait_send()
        docs_out = emb.at[pl.ds(0, doc_part), :]
        pltpu.make_async_remote_copy(
            src_ref=docs_out, dst_ref=docs_out, send_sem=doc_send.at[k], recv_sem=doc_recv.at[0, 0, 0],
            device_id={"dp": device(z, turn(x, k, nx), core)}, device_id_type=MESH,
        ).wait_send()
        for e in range(1, n_ens):
            pltpu.make_async_remote_copy(
                src_ref=docs_out, dst_ref=docs_out, send_sem=fwd_send.at[k, e], recv_sem=doc_recv.at[0, 0, 0],
                device_id={"ens": turn(ens, e, n_ens)}, device_id_type=MESH,
            ).wait_send()
    for place in range(n_chips):
        zo, xo = divmod(place, nx)
        for s in (1, -1):
            @pl.when((z + s >= 0) & (z + s < nz) & ((zo <= z) if s > 0 else (zo >= z)))
            def _():
                whole = w.at[:, origin_rows(device(zo, xo, core)), :]
                pltpu.make_async_remote_copy(
                    src_ref=whole, dst_ref=whole,
                    send_sem=z_send.at[0 if s > 0 else 1, place], recv_sem=w_recv.at[0, 0],
                    device_id={"dp": me + s * nx * nc}, device_id_type=MESH,
                ).wait_send()
    for k in range(1, nc):
        blocks = w.at[:, pl.ds(0, n_chips * rows), :]
        pltpu.make_async_remote_copy(
            src_ref=blocks, dst_ref=blocks, send_sem=core_send.at[k], recv_sem=core_recv.at[0, k],
            device_id={"dp": device(z, x, turn(core, k, nc))}, device_id_type=MESH,
        ).wait_send()
    for k, e in others:
        sc_copy(k, e).wait_send()
    for b in range(PARTS):
        for k in range(1, nx):
            px_copy(k, b).wait_send()
        for e in range(1, n_ens):
            part_copy(e, b).wait_send()
    all_tot.wait_send()


def solution(mesh):
    geo = geometry(mesh)
    nz, nx, nc = geo
    n_dp, n_ens = mesh.shape["dp"], mesh.shape["ens"]

    def on_device(embeddings, valid_mask, first_weight, second_weight, thresholds):
        docs, width = embeddings.shape
        members, rows, units = first_weight.shape
        classes = second_weight.shape[2]
        share = units // nx
        cols = min(COLS, share)
        chunks = members * share // cols
        own = members // n_ens
        lines = -(-members // 8) * 8
        dma = pltpu.SemaphoreType.DMA
        hbm, vmem, smem = (pl.BlockSpec(memory_space=s) for s in (pl.ANY, pltpu.VMEM, pltpu.SMEM))
        mean_logits, shares = pl.pallas_call(
            functools.partial(kernel, geo, n_ens),
            out_shape=(
                pltpu.VMEM((docs, classes), jnp.float32),
                pltpu.SMEM((2 * own,), jnp.float32),
            ),
            in_specs=[hbm] * 5,
            out_specs=(vmem, smem),
            scratch_shapes=[
                pltpu.VMEM((chunks, width, cols), jnp.bfloat16),
                pltpu.VMEM((nx * docs, width), jnp.bfloat16),
                pltpu.VMEM((members, share, classes), jnp.bfloat16),
                pltpu.VMEM((members, nx * docs, classes), jnp.float32),
                pltpu.VMEM((nx * docs, cols), jnp.bfloat16),
                pltpu.VMEM(valid_mask.shape, valid_mask.dtype),
                pltpu.SMEM(thresholds.shape, thresholds.dtype),
                pltpu.VMEM((nx, docs, classes), jnp.bfloat16),
                pltpu.VMEM((nx, docs, classes), jnp.bfloat16),
                pltpu.VMEM((n_ens, docs, classes), jnp.bfloat16),
                pltpu.VMEM((nx, lines, docs), jnp.float32),
                pltpu.VMEM((nx * n_ens, lines, docs), jnp.float32),
                pltpu.VMEM((n_dp, lines, 128), jnp.float32),
                dma((chunks,)),
                dma((4,)),
                dma((2, nz * nx)),
                dma((nz * nx, chunks)),
                dma((nx,)),
                dma((nc,)),
                dma((chunks, nc)),
                dma((nx,)),
                dma((nx, n_ens, PIECES)),
                dma((nx, n_ens)),
                dma((nx, PARTS)),
                dma((nx, PARTS)),
                dma((n_ens, PARTS)),
                dma((n_ens, PARTS)),
                dma((nx, n_ens)),
                dma((nx * n_ens,)),
                dma((2,)),
            ],
            compiler_params=pltpu.CompilerParams(
                collective_id=0, has_side_effects=True, vmem_limit_bytes=63 * 1024 * 1024
            ),
        )(embeddings, valid_mask, first_weight, second_weight, thresholds)
        return mean_logits, shares[:own], shares[own:]

    return jax.shard_map(
        on_device,
        mesh=mesh,
        in_specs=(P("dp", None), P("dp"), P(None, "dp", "ens"), P(None, "ens", None), P()),
        out_specs=(P("dp", None), P("ens"), P("ens")),
        check_vma=False,
    )
```

time: 69.8 us -> 61.6 us (0.88)
  Pallas kernels: 63.6 us -> 59.5 us
  between operations: 4.21 us -> 0.64 us
    pallas_call x1, Pallas kernels: 63.6 us -> 59.5 us  [on_device(): pl.pallas_call(functools.partial(kernel, geo, n_ens), out_shape=(pltpu.VM...]
    unnamed x1, local copies, waits for them, and re-layouts: 1.77 us -> 0.75 us
where the time goes in v1:
time: 61.6 us; the launch traced here: 61.5 us
  Pallas kernels  59.5 us (97%)
  local copies, waits for them, and re-layouts  1.35 us (2%)
  between operations  0.64 us (1%)
    pallas_call x1, Pallas kernels, on_device(): pl.pallas_call(functools.partial(kernel, geo, n_ens), out_shape=(pltpu.VM...  59.5 us

profile of v1, /device:TPU:0, one launch (start us, length us, event | category | flops | bytes accessed | tf_op | source)
XLA Modules:
  0.0 61.5 jit_solution(3833882720338894695)
XLA Ops:
  0.6 59.5 %shard_map.76 = (f32[768,128]{1,0:T(8,128)S(1)}, f32[2]{0:T(128)S(4)}) custom-call(bf16[768,1024]{1,0:T(8,128)(2,1)} %emb_hbm.1, s32[768]{0:T(1024)} %mask_hbm.1, bf16[2,64,2048]{2,1,0:T(8,128)(2,1)} %fw_hbm.1, bf16[2,2048,128]{2,1,0:T(8,128)(2,1)} %sw_hbm.1, s32[2]{0:T(128)} %thr_hbm.1), custom_call_target="tpu_custom_call" | custom-call | tf_op jit(solution)/shard_map/pallas_call | solution.py:484
  60.1 0.7 %copy.9 = f32[768,128]{1,0:T(8,128)} copy(f32[768,128]{1,0:T(8,128)S(1)} %get-tuple-element.9) | data formatting | bytes 786432
  60.9 0.6 fusion

commit v2 on v1

--- a/solution.py
+++ b/solution.py
@@ -11,8 +11,9 @@
 MESH = pl.DeviceIdType.MESH
 COLS = 256
 ROWS = 256
-PIECES = 4
-PARTS = 4
+PIECES = 8
+EARLY = 2
+SPLIT = 2
 
 
 def geometry(mesh):
@@ -29,7 +30,7 @@
 
 def kernel(
     geo, n_ens, emb_hbm, mask_hbm, fw_hbm, sw_hbm, thr_hbm, out_ref, share_ref,
-    w, emb, sw, acc, hid, mask, thr, px_out, px_in, part, sc_out, sc_in, tot,
+    w, emb, sw, acc, hid, pre, mask, thr, px_out, px_in, part, sc_out, sc_in, tot,
     local_sem, load_sem, z_send, w_recv, x_send, core_send, core_recv, doc_send, doc_recv, fwd_send,
     px_send, px_recv, part_send, part_recv, sc_send, sc_recv, tot_sem,
 ):
@@ -42,14 +43,24 @@
     share = units // nx
     docs, classes = out_ref.shape
     doc_part = docs // n_ens
-    doc_piece = doc_part // PIECES
+    pieces = doc_recv.shape[2]
+    doc_piece = doc_part // pieces
     step_rows = math.gcd(docs, ROWS)
+    n_blocks = docs // step_rows
+    piece_rows = step_rows // SPLIT
+    n_parts = docs // piece_rows
+    final = chunks - 1
+    plane = nx * nc * rows
+    early = min(EARLY, chunks - 1)
 
     me = lax.axis_index("dp")
     ens = lax.axis_index("ens")
     core = lax.rem(me, nc)
     chip = me // nc
     z, x = chip // nx, lax.rem(chip, nx)
+    far = jnp.where(2 * z < nz, nz - 1, 0)
+    near_cols = pl.ds(pl.multiple_of(jnp.where(far == 0, plane, 0), plane), width - plane)
+    far_cols = pl.ds(pl.multiple_of(far * plane, plane), plane)
 
     def device(zz, xx, cc):
         return (zz * nx + xx) * nc + cc
@@ -157,7 +168,7 @@
     def core_copy(c, zo, xo, k):
         return pltpu.make_async_remote_copy(
             src_ref=block(c, zo, xo), dst_ref=block(c, zo, xo),
-            send_sem=core_send.at[k], recv_sem=core_recv.at[c, k],
+            send_sem=core_send.at[k], recv_sem=core_recv.at[c, k, jnp.where(zo == far, 1, 0)],
             device_id={"dp": device(z, x, turn(core, k, nc))}, device_id_type=MESH,
         )
 
@@ -176,16 +187,16 @@
             device_id={"dp": me}, device_id_type=MESH,
         ).wait_recv()
 
-    def from_cores(c, k):
-        blocks = w.at[c, pl.ds(0, n_chips * rows), :]
-        return pltpu.make_async_remote_copy(
-            src_ref=blocks, dst_ref=blocks, send_sem=core_send.at[k], recv_sem=core_recv.at[c, k],
+    def from_cores(c, k, is_far):
+        blocks = w.at[c, pl.ds(0, (nx if is_far else n_chips - nx) * rows), :]
+        return pltpu.make_async_remote_copy(
+            src_ref=blocks, dst_ref=blocks, send_sem=core_send.at[k], recv_sem=core_recv.at[c, k, is_far],
             device_id={"dp": device(z, x, turn(core, k, nc))}, device_id_type=MESH,
         )
 
     for k in range(1, nx):
         loop(chunks, lambda c: x_weights(k, c).start())
-        for i in range(PIECES):
+        for i in range(pieces):
             x_docs(k, i).start()
 
     def first(c):
@@ -218,54 +229,130 @@
             for e in range(1, n_ens):
                 doc_forward(k, i, e).start()
 
-    sent = 0
+    step_bytes = nx * rows * cols
+    share_bytes = (nx - 1) * chunks * rows * cols
+    due = {}
+    for i in range(pieces):
+        at = -(-(share_bytes + (nx - 1) * (i + 1) * doc_piece * width) // step_bytes)
+        due.setdefault(min(at, (nz - 2) * chunks - 1), []).append(i)
     for d in range(1, nz - 1):
-        due = {chunks - 1: [0]} if d == 1 else {}
-        if d == 2:
-            for i in range(1, PIECES):
-                due.setdefault((i * chunks) // (PIECES - 1) - 1, []).append(i)
-
         def relay(c):
             take(d, c)
-            for at, pieces in due.items():
-                @pl.when(c == at)
-                def _():
-                    for i in pieces:
-                        forward_docs(i)
+            for at, ready in due.items():
+                if at // chunks == d - 1:
+                    @pl.when(c == at % chunks)
+                    def _():
+                        for i in ready:
+                            forward_docs(i)
         loop(chunks, relay)
-        sent += sum(len(v) for v in due.values())
-    for i in range(sent, PIECES):
-        forward_docs(i)
+    if nz < 3:
+        for i in range(pieces):
+            forward_docs(i)
+    for copy in (emb_copy, sw_copy, mask_copy, thr_copy):
+        copy.wait()
+
+    def last_take(c):
+        if nz > 1:
+            take(nz - 1, c)
+
+    def cores_arrived(c, sides):
+        for k in range(1, nc):
+            for is_far in sides:
+                if is_far or nz > 1:
+                    from_cores(c, k, is_far).wait_recv()
+
+    def layer_one(c, row, into):
+        hid[row, into] = jnp.maximum(
+            jnp.dot(emb[row, :], w[c], preferred_element_type=jnp.float32), 0.0
+        ).astype(jnp.bfloat16)
+
+    def member_rows(c, n=1):
+        m = c // per_member
+        return m, pl.ds(pl.multiple_of(lax.rem(c, per_member) * cols, cols), n * cols)
+
+    def slot_block(k, r):
+        return pl.ds(pl.multiple_of(turn(x, k, nx) * docs + r * step_rows, step_rows), step_rows)
+
+    def early_slot(k):
+        for c in range(early):
+            for r in range(n_blocks):
+                layer_one(c, slot_block(k, r), pl.ds(c * cols, cols))
+        row = slot(turn(x, k, nx))
+        for c in range(early):
+            m, at = member_rows(c)
+            acc[m, row, :] += jnp.dot(
+                hid[row, pl.ds(c * cols, cols)], sw[m, at, :], preferred_element_type=jnp.float32
+            )
+
+    def compute(c):
+        cores_arrived(c, (0, 1))
+        for r in range(0, nx * docs, step_rows):
+            layer_one(c, pl.ds(r, step_rows), pl.ds(0, cols))
+        m, at = member_rows(c)
+        acc[m] += jnp.dot(hid[:, 0:cols], sw[m, at, :], preferred_element_type=jnp.float32)
+
+    def near_slot(k):
+        for r in range(n_blocks):
+            row = slot_block(k, r)
+            if nz > 1:
+                pre[row, :] = jnp.dot(emb[row, near_cols], w[final, near_cols, :], preferred_element_type=jnp.float32)
+            else:
+                pre[row, :] = jnp.zeros((step_rows, cols), jnp.float32)
+
+    def far_block(k, r):
+        row = slot_block(k, r)
+        total = pre[row, :] + jnp.dot(emb[row, far_cols], w[final, far_cols, :], preferred_element_type=jnp.float32)
+        hid[row, 0:cols] = jnp.maximum(total, 0.0).astype(jnp.bfloat16)
+
+    cores_arrived(final, (0,))
+    near_slot(0)
+    loop(early, last_take)
+    for c in range(early):
+        cores_arrived(c, (0, 1))
+    early_slot(0)
+    last_take(early)
     for k in range(1, nx):
         for e in range(1, n_ens):
-            for i in range(PIECES):
+            for i in range(pieces):
                 doc_arrived(k, i, e)
-    for copy in (emb_copy, sw_copy, mask_copy, thr_copy):
-        copy.wait()
-
-    def compute(c):
-        for k in range(1, nc):
-            from_cores(c, k).wait_recv()
-        m = c // per_member
-        at = pl.ds(pl.multiple_of(lax.rem(c, per_member) * cols, cols), cols)
-        for r in range(0, nx * docs, step_rows):
-            hid[pl.ds(r, step_rows), :] = jnp.maximum(
-                jnp.dot(emb[pl.ds(r, step_rows), :], w[c], preferred_element_type=jnp.float32), 0.0
-            ).astype(jnp.bfloat16)
-        acc[m] += jnp.dot(hid[...], sw[m, at, :], preferred_element_type=jnp.float32)
-
-    def last(c):
-        if nz > 1:
-            @pl.when(c < chunks)
-            def _():
-                take(nz - 1, c)
-
-        @pl.when(c > 0)
-        def _():
-            compute(c - 1)
-    loop(chunks + 1, last)
-
-    lines = sc_in.shape[1]
+    for k in range(1, nx):
+        early_slot(k)
+        near_slot(k)
+
+    def middle(i):
+        last_take(i + early + 1)
+        compute(i + early)
+    loop(chunks - early - 1, middle)
+
+    cores_arrived(final, (1,))
+    final_m, final_at = member_rows(final)
+
+    def piece_of(b):
+        return pl.ds(b * piece_rows, piece_rows)
+
+    def mean_part(k, b):
+        row = pl.ds(pl.multiple_of(turn(x, k, nx) * docs + b * piece_rows, piece_rows), piece_rows)
+        total = acc[0, row, :]
+        for m in range(1, members):
+            total += acc[m, row, :]
+        return total * (1.0 / members)
+
+    def px_copy(k, b):
+        return pltpu.make_async_remote_copy(
+            src_ref=px_out.at[k, piece_of(b), :], dst_ref=px_in.at[x, piece_of(b), :],
+            send_sem=px_send.at[k, b], recv_sem=px_recv.at[x, b],
+            device_id={"dp": device(z, turn(x, k, nx), core)}, device_id_type=MESH,
+        )
+
+    for k in range(1, nx):
+        for r in range(n_blocks):
+            row = slot_block(k, r)
+            far_block(k, r)
+            acc[final_m, row, :] += jnp.dot(
+                hid[row, 0:cols], sw[final_m, final_at, :], preferred_element_type=jnp.float32
+            )
+
+    lines = -(-members // 8) * 8
     wide = members * classes
     lane = lax.broadcasted_iota(jnp.int32, (lines, wide), 1)
     line = lax.broadcasted_iota(jnp.int32, (lines, wide), 0)
@@ -283,7 +370,7 @@
         dims = (((1,), (1,)), ((), ()))
         s = lax.dot_general(g, hi, dims, preferred_element_type=jnp.float32)
         s += lax.dot_general(g, lo, dims, preferred_element_type=jnp.float32)
-        return s[:lines] + s[lines:]
+        return s[:members] + s[lines : lines + members]
 
     mine = x * n_ens + ens
 
@@ -303,9 +390,8 @@
             device_id={"dp": me}, device_id_type=MESH,
         ).wait_recv()
 
-    for k in list(range(1, nx)) + [0]:
-        xp = turn(x, k, nx)
-        s = scores_of(xp)
+    def send_scores(k):
+        s = scores_of(turn(x, k, nx))
         sc_out[k] = s
         if k == 0:
             sc_in[mine] = s
@@ -313,22 +399,17 @@
             if k or e:
                 sc_copy(k, e).start()
 
-    def piece_of(b):
-        return pl.ds(b * (docs // PARTS), docs // PARTS)
-
-    def mean_part(xp, b):
-        rows_b = pl.ds(pl.multiple_of(xp * docs + b * (docs // PARTS), docs // PARTS), docs // PARTS)
-        total = acc[0, rows_b, :]
-        for m in range(1, members):
-            total += acc[m, rows_b, :]
-        return total * (1.0 / members)
-
-    def px_copy(k, b):
-        return pltpu.make_async_remote_copy(
-            src_ref=px_out.at[k, piece_of(b), :], dst_ref=px_in.at[x, piece_of(b), :],
-            send_sem=px_send.at[k, b], recv_sem=px_recv.at[x, b],
-            device_id={"dp": device(z, turn(x, k, nx), core)}, device_id_type=MESH,
-        )
+    for k in range(1, nx):
+        send_scores(k)
+        for b in range(n_parts):
+            px_out[k, piece_of(b), :] = mean_part(k, b).astype(jnp.bfloat16)
+            px_copy(k, b).start()
+    for r in range(n_blocks):
+        far_block(0, r)
+    acc[final_m, slot(x), :] += jnp.dot(
+        hid[slot(x), 0:cols], sw[final_m, final_at, :], preferred_element_type=jnp.float32
+    )
+    send_scores(0)
 
     def px_arrived(k, b):
         xp = turn(x, k, nx)
@@ -345,13 +426,8 @@
             device_id={"ens": turn(ens, e, n_ens)}, device_id_type=MESH,
         )
 
-    for b in range(PARTS):
-        for k in range(1, nx):
-            px_out[k, piece_of(b), :] = mean_part(turn(x, k, nx), b).astype(jnp.bfloat16)
-            px_copy(k, b).start()
-
     def relay_part(b):
-        total = mean_part(x, b)
+        total = mean_part(0, b)
         for k in range(1, nx):
             px_arrived(k, b)
             total += px_in[turn(x, k, nx), piece_of(b), :].astype(jnp.float32)
@@ -359,14 +435,15 @@
         for e in range(1, n_ens):
             part_copy(e, b).start()
 
-    relay_part(0)
+    for b in range(1):
+        relay_part(b)
     for k, e in others:
         sc_arrived(k, e)
     scores = sc_in[0]
     for k in range(1, nx * n_ens):
         scores += sc_in[k]
-    row = lax.broadcasted_iota(jnp.int32, (lines, docs), 0)
-    cutoff = jnp.zeros((lines, docs), jnp.float32)
+    row = lax.broadcasted_iota(jnp.int32, (members, docs), 0)
+    cutoff = jnp.zeros((members, docs), jnp.float32)
     mean_cutoff = jnp.float32(0.0)
     for m in range(members):
         level = thr[m].astype(jnp.float32) * (1.0 / 256.0)
@@ -377,8 +454,10 @@
     ens_kept = jax.nn.sigmoid(4.0 * (ens_score - mean_cutoff))
     kept_sum = jnp.sum(kept, axis=1, keepdims=True)
     agree_sum = jnp.sum(kept * ens_kept, axis=1, keepdims=True)
-    lane = lax.broadcasted_iota(jnp.int32, (lines, 128), 1)
-    tot[me] = jnp.where(lane == 0, kept_sum, jnp.where(lane == 1, agree_sum, 0.0))
+    lane = lax.broadcasted_iota(jnp.int32, (members, 128), 1)
+    line = lax.broadcasted_iota(jnp.int32, (members, 128), 0)
+    spread = jnp.where(lane == line, kept_sum, 0.0) + jnp.where(lane == line + members, agree_sum, 0.0)
+    tot[me] = jnp.sum(spread, axis=0, keepdims=True)
 
     def tot_copy(k):
         return pltpu.make_async_remote_copy(
@@ -394,10 +473,10 @@
     for k in range(1, n_dp):
         tot_copy(k).start()
 
-    for b in range(1, PARTS):
+    for b in range(1, n_parts):
         relay_part(b)
 
-    for b in range(PARTS):
+    for b in range(n_parts):
         for e in range(1, n_ens):
             other = turn(ens, e, n_ens)
             block_in = part.at[other, piece_of(b), :]
@@ -416,11 +495,10 @@
         sums += tot[k]
     sums = sums / docs
     own = members // n_ens
-    row = lax.broadcasted_iota(jnp.int32, (lines, 128), 0)
+    lane = lax.broadcasted_iota(jnp.int32, sums.shape, 1)
     for j in range(own):
-        hit = row == ens * own + j
         for i in range(2):
-            share_ref[i * own + j] = jnp.sum(jnp.where(hit & (lane == i), sums, 0.0))
+            share_ref[i * own + j] = jnp.sum(jnp.where(lane == i * members + ens * own + j, sums, 0.0))
 
     for k in range(1, nx):
         whole = w.at[:, origin_rows(me), :]
@@ -452,12 +530,12 @@
     for k in range(1, nc):
         blocks = w.at[:, pl.ds(0, n_chips * rows), :]
         pltpu.make_async_remote_copy(
-            src_ref=blocks, dst_ref=blocks, send_sem=core_send.at[k], recv_sem=core_recv.at[0, k],
+            src_ref=blocks, dst_ref=blocks, send_sem=core_send.at[k], recv_sem=core_recv.at[0, k, 0],
             device_id={"dp": device(z, x, turn(core, k, nc))}, device_id_type=MESH,
         ).wait_send()
     for k, e in others:
         sc_copy(k, e).wait_send()
-    for b in range(PARTS):
+    for b in range(n_parts):
         for k in range(1, nx):
             px_copy(k, b).wait_send()
         for e in range(1, n_ens):
@@ -478,7 +556,9 @@
         cols = min(COLS, share)
         chunks = members * share // cols
         own = members // n_ens
-        lines = -(-members // 8) * 8
+        early = min(EARLY, chunks - 1)
+        parts = docs // math.gcd(docs, ROWS) * SPLIT
+        pieces = math.gcd(docs // n_ens // 16, PIECES)
         dma = pltpu.SemaphoreType.DMA
         hbm, vmem, smem = (pl.BlockSpec(memory_space=s) for s in (pl.ANY, pltpu.VMEM, pltpu.SMEM))
         mean_logits, shares = pl.pallas_call(
@@ -494,29 +574,30 @@
                 pltpu.VMEM((nx * docs, width), jnp.bfloat16),
                 pltpu.VMEM((members, share, classes), jnp.bfloat16),
                 pltpu.VMEM((members, nx * docs, classes), jnp.float32),
-                pltpu.VMEM((nx * docs, cols), jnp.bfloat16),
+                pltpu.VMEM((nx * docs, early * cols), jnp.bfloat16),
+                pltpu.VMEM((nx * docs, cols), jnp.float32),
                 pltpu.VMEM(valid_mask.shape, valid_mask.dtype),
                 pltpu.SMEM(thresholds.shape, thresholds.dtype),
                 pltpu.VMEM((nx, docs, classes), jnp.bfloat16),
                 pltpu.VMEM((nx, docs, classes), jnp.bfloat16),
                 pltpu.VMEM((n_ens, docs, classes), jnp.bfloat16),
-                pltpu.VMEM((nx, lines, docs), jnp.float32),
-                pltpu.VMEM((nx * n_ens, lines, docs), jnp.float32),
-                pltpu.VMEM((n_dp, lines, 128), jnp.float32),
+                pltpu.VMEM((nx, members, docs), jnp.float32),
+                pltpu.VMEM((nx * n_ens, members, docs), jnp.float32),
+                pltpu.VMEM((n_dp, 1, 128), jnp.float32),
                 dma((chunks,)),
                 dma((4,)),
                 dma((2, nz * nx)),
                 dma((nz * nx, chunks)),
                 dma((nx,)),
                 dma((nc,)),
-                dma((chunks, nc)),
+                dma((chunks, nc, 2)),
                 dma((nx,)),
-                dma((nx, n_ens, PIECES)),
+                dma((nx, n_ens, pieces)),
                 dma((nx, n_ens)),
-                dma((nx, PARTS)),
-                dma((nx, PARTS)),
-                dma((n_ens, PARTS)),
-                dma((n_ens, PARTS)),
+                dma((nx, parts)),
+                dma((nx, parts)),
+                dma((n_ens, parts)),
+                dma((n_ens, parts)),
                 dma((nx, n_ens)),
                 dma((nx * n_ens,)),
                 dma((2,)),

time: 61.6 us -> 57.6 us (0.935)
  Pallas kernels: 59.5 us -> 55.5 us
    pallas_call x1, Pallas kernels: 59.5 us -> 55.5 us  [on_device(): pl.pallas_call(functools.partial(kernel, geo, n_ens), out_shape=(pltpu.VM...]
where the time goes in v2:
time: 57.6 us; the launch traced here: 57.5 us
  Pallas kernels  55.5 us (96%)
  local copies, waits for them, and re-layouts  1.35 us (2%)
  between operations  0.64 us (1%)
    pallas_call x1, Pallas kernels, on_device(): pl.pallas_call(functools.partial(kernel, geo, n_ens), out_shape=(pltpu.VM...  55.5 us

profile of v2, /device:TPU:0, one launch (start us, length us, event | category | flops | bytes accessed | tf_op | source)
XLA Modules:
  0.0 57.5 jit_solution(7192860864092561689)
XLA Ops:
  0.6 55.5 %shard_map.76 = (f32[768,128]{1,0:T(8,128)S(1)}, f32[2]{0:T(128)S(4)}) custom-call(bf16[768,1024]{1,0:T(8,128)(2,1)} %emb_hbm.1, s32[768]{0:T(1024)} %mask_hbm.1, bf16[2,64,2048]{2,1,0:T(8,128)(2,1)} %fw_hbm.1, bf16[2,2048,128]{2,1,0:T(8,128)(2,1)} %sw_hbm.1, s32[2]{0:T(128)} %thr_hbm.1), custom_call_target="tpu_custom_call" | custom-call | tf_op jit(solution)/shard_map/pallas_call | solution.py:564
  56.1 0.7 %copy.9 = f32[768,128]{1,0:T(8,128)} copy(f32[768,128]{1,0:T(8,128)S(1)} %get-tuple-element.9) | data formatting | bytes 786432
  56.8 0.6 %fusion = (f32[1]{0:T(128)}, f32[1]{0:T(128)}) fusion(f32[2]{0:T(128)S(4)} %get-tuple-element.6), kind=kLoop, calls=%fused_computation | loop fusion | bytes 16 | tf_op jit(solution)/shard_map/slice | solution.py:609

commit v3 on v2

--- a/solution.py
+++ b/solution.py
@@ -9,11 +9,12 @@
 from jax.sharding import PartitionSpec as P
 
 MESH = pl.DeviceIdType.MESH
-COLS = 256
-ROWS = 256
-PIECES = 8
-EARLY = 2
+COLS = 512
+ROWS = 384
+PIECES = 12
+EARLY = 1
 SPLIT = 2
+AHEAD = 1
 
 
 def geometry(mesh):
@@ -58,6 +59,7 @@
     core = lax.rem(me, nc)
     chip = me // nc
     z, x = chip // nx, lax.rem(chip, nx)
+    inner = (z > 0) & (z < nz - 1)
     far = jnp.where(2 * z < nz, nz - 1, 0)
     near_cols = pl.ds(pl.multiple_of(jnp.where(far == 0, plane, 0), plane), width - plane)
     far_cols = pl.ds(pl.multiple_of(far * plane, plane), plane)
@@ -229,6 +231,92 @@
             for e in range(1, n_ens):
                 doc_forward(k, i, e).start()
 
+    def last_take(c):
+        if nz > 1:
+            take(nz - 1, c)
+
+    def cores_arrived(c, sides):
+        for k in range(1, nc):
+            for is_far in sides:
+                if is_far or nz > 1:
+                    from_cores(c, k, is_far).wait_recv()
+
+    def layer_one(c, row, into):
+        hid[row, into] = jnp.maximum(
+            jnp.dot(emb[row, :], w[c], preferred_element_type=jnp.float32), 0.0
+        ).astype(jnp.bfloat16)
+
+    def member_rows(c, n=1):
+        m = c // per_member
+        return m, pl.ds(pl.multiple_of(lax.rem(c, per_member) * cols, cols), n * cols)
+
+    def slot_block(k, r):
+        return pl.ds(pl.multiple_of(turn(x, k, nx) * docs + r * step_rows, step_rows), step_rows)
+
+    def near_block(at, c, k, r):
+        if nz > 1:
+            row = slot_block(k, r)
+            pre[at, pl.ds(r * step_rows, step_rows), :] = jnp.dot(
+                emb[row, near_cols], w[c, near_cols, :], preferred_element_type=jnp.float32
+            )
+        else:
+            pre[at, pl.ds(r * step_rows, step_rows), :] = jnp.zeros((step_rows, cols), jnp.float32)
+
+    def near_own(c):
+        cores_arrived(c, (0,))
+        for r in range(n_blocks):
+            near_block(c, c, 0, r)
+
+    def far_block(at, c, k, r, into):
+        row = slot_block(k, r)
+        total = pre[at, pl.ds(r * step_rows, step_rows), :] + jnp.dot(
+            emb[row, far_cols], w[c, far_cols, :], preferred_element_type=jnp.float32
+        )
+        hid[row, into] = jnp.maximum(total, 0.0).astype(jnp.bfloat16)
+
+    def layer_two(c, k, into):
+        m, at = member_rows(c)
+        row = slot(turn(x, k, nx))
+        acc[m, row, :] += jnp.dot(hid[row, into], sw[m, at, :], preferred_element_type=jnp.float32)
+
+    def early_slot(k):
+        for c in range(early):
+            for r in range(n_blocks):
+                if k == 0:
+                    far_block(c, c, 0, r, pl.ds(c * cols, cols))
+                else:
+                    layer_one(c, slot_block(k, r), pl.ds(c * cols, cols))
+        for c in range(early):
+            layer_two(c, k, pl.ds(c * cols, cols))
+
+    def own_chunk(c):
+        cores_arrived(c, (1,))
+        for r in range(n_blocks):
+            far_block(c, c, 0, r, pl.ds(0, cols))
+        layer_two(c, 0, pl.ds(0, cols))
+
+    def compute(c):
+        @pl.when(jnp.logical_not(inner))
+        def _():
+            cores_arrived(c, (1,))
+            for k in range(nx):
+                for r in range(n_blocks):
+                    if k == 0:
+                        far_block(c, c, 0, r, pl.ds(0, cols))
+                    else:
+                        layer_one(c, slot_block(k, r), pl.ds(0, cols))
+            m, at = member_rows(c)
+            acc[m] += jnp.dot(hid[:, 0:cols], sw[m, at, :], preferred_element_type=jnp.float32)
+
+        @pl.when(inner)
+        def _():
+            for k in range(1, nx):
+                for r in range(n_blocks):
+                    layer_one(c, slot_block(k, r), pl.ds(0, cols))
+                layer_two(c, k, pl.ds(0, cols))
+
+    for copy in (emb_copy, sw_copy, mask_copy, thr_copy):
+        copy.wait()
     step_bytes = nx * rows * cols
     share_bytes = (nx - 1) * chunks * rows * cols
     due = {}
@@ -244,80 +332,33 @@
                     def _():
                         for i in ready:
                             forward_docs(i)
+            if d == nz - 2:
+                @pl.when(c > 0)
+                def _():
+                    near_own(c - 1)
         loop(chunks, relay)
     if nz < 3:
+        loop(final, near_own)
         for i in range(pieces):
             forward_docs(i)
-    for copy in (emb_copy, sw_copy, mask_copy, thr_copy):
-        copy.wait()
-
-    def last_take(c):
-        if nz > 1:
-            take(nz - 1, c)
-
-    def cores_arrived(c, sides):
-        for k in range(1, nc):
-            for is_far in sides:
-                if is_far or nz > 1:
-                    from_cores(c, k, is_far).wait_recv()
-
-    def layer_one(c, row, into):
-        hid[row, into] = jnp.maximum(
-            jnp.dot(emb[row, :], w[c], preferred_element_type=jnp.float32), 0.0
-        ).astype(jnp.bfloat16)
-
-    def member_rows(c, n=1):
-        m = c // per_member
-        return m, pl.ds(pl.multiple_of(lax.rem(c, per_member) * cols, cols), n * cols)
-
-    def slot_block(k, r):
-        return pl.ds(pl.multiple_of(turn(x, k, nx) * docs + r * step_rows, step_rows), step_rows)
-
-    def early_slot(k):
-        for c in range(early):
-            for r in range(n_blocks):
-                layer_one(c, slot_block(k, r), pl.ds(c * cols, cols))
-        row = slot(turn(x, k, nx))
-        for c in range(early):
-            m, at = member_rows(c)
-            acc[m, row, :] += jnp.dot(
-                hid[row, pl.ds(c * cols, cols)], sw[m, at, :], preferred_element_type=jnp.float32
-            )
-
-    def compute(c):
-        cores_arrived(c, (0, 1))
-        for r in range(0, nx * docs, step_rows):
-            layer_one(c, pl.ds(r, step_rows), pl.ds(0, cols))
-        m, at = member_rows(c)
-        acc[m] += jnp.dot(hid[:, 0:cols], sw[m, at, :], preferred_element_type=jnp.float32)
-
-    def near_slot(k):
-        for r in range(n_blocks):
-            row = slot_block(k, r)
-            if nz > 1:
-                pre[row, :] = jnp.dot(emb[row, near_cols], w[final, near_cols, :], preferred_element_type=jnp.float32)
-            else:
-                pre[row, :] = jnp.zeros((step_rows, cols), jnp.float32)
-
-    def far_block(k, r):
-        row = slot_block(k, r)
-        total = pre[row, :] + jnp.dot(emb[row, far_cols], w[final, far_cols, :], preferred_element_type=jnp.float32)
-        hid[row, 0:cols] = jnp.maximum(total, 0.0).astype(jnp.bfloat16)
-
-    cores_arrived(final, (0,))
-    near_slot(0)
+    near_own(final)
     loop(early, last_take)
     for c in range(early):
-        cores_arrived(c, (0, 1))
+        cores_arrived(c, (1,))
     early_slot(0)
     last_take(early)
+
+    @pl.when(inner)
+    def _():
+        loop(chunks - early - 1, lambda i: own_chunk(i + early))
     for k in range(1, nx):
         for e in range(1, n_ens):
             for i in range(pieces):
                 doc_arrived(k, i, e)
     for k in range(1, nx):
         early_slot(k)
-        near_slot(k)
+        for r in range(n_blocks):
+            near_block(chunks + k - 1, final, k, r)
 
     def middle(i):
         last_take(i + early + 1)
@@ -344,13 +385,20 @@
             device_id={"dp": device(z, turn(x, k, nx), core)}, device_id_type=MESH,
         )
 
+    def send_parts(k, pieces_of_k):
+        for b in pieces_of_k:
+            px_out[k, piece_of(b), :] = mean_part(k, b).astype(jnp.bfloat16)
+            px_copy(k, b).start()
+
     for k in range(1, nx):
         for r in range(n_blocks):
             row = slot_block(k, r)
-            far_block(k, r)
+            far_block(chunks + k - 1, final, k, r, pl.ds(0, cols))
             acc[final_m, row, :] += jnp.dot(
                 hid[row, 0:cols], sw[final_m, final_at, :], preferred_element_type=jnp.float32
             )
+            if r == 0:
+                send_parts(k, range(AHEAD))
 
     lines = -(-members // 8) * 8
     wide = members * classes
@@ -401,11 +449,9 @@
 
     for k in range(1, nx):
         send_scores(k)
-        for b in range(n_parts):
-            px_out[k, piece_of(b), :] = mean_part(k, b).astype(jnp.bfloat16)
-            px_copy(k, b).start()
+        send_parts(k, range(AHEAD, n_parts))
     for r in range(n_blocks):
-        far_block(0, r)
+        far_block(final, final, 0, r, pl.ds(0, cols))
     acc[final_m, slot(x), :] += jnp.dot(
         hid[slot(x), 0:cols], sw[final_m, final_at, :], preferred_element_type=jnp.float32
     )
@@ -434,71 +480,6 @@
         part[ens, piece_of(b), :] = total.astype(jnp.bfloat16)
         for e in range(1, n_ens):
             part_copy(e, b).start()
-
-    for b in range(1):
-        relay_part(b)
-    for k, e in others:
-        sc_arrived(k, e)
-    scores = sc_in[0]
-    for k in range(1, nx * n_ens):
-        scores += sc_in[k]
-    row = lax.broadcasted_iota(jnp.int32, (members, docs), 0)
-    cutoff = jnp.zeros((members, docs), jnp.float32)
-    mean_cutoff = jnp.float32(0.0)
-    for m in range(members):
-        level = thr[m].astype(jnp.float32) * (1.0 / 256.0)
-        cutoff = jnp.where(row == m, level, cutoff)
-        mean_cutoff += level * (1.0 / members)
-    kept = mask[...].reshape(1, docs).astype(jnp.float32) * jax.nn.sigmoid(4.0 * (scores - cutoff))
-    ens_score = jnp.sum(scores, axis=0, keepdims=True) * (1.0 / members)
-    ens_kept = jax.nn.sigmoid(4.0 * (ens_score - mean_cutoff))
-    kept_sum = jnp.sum(kept, axis=1, keepdims=True)
-    agree_sum = jnp.sum(kept * ens_kept, axis=1, keepdims=True)
-    lane = lax.broadcasted_iota(jnp.int32, (members, 128), 1)
-    line = lax.broadcasted_iota(jnp.int32, (members, 128), 0)
-    spread = jnp.where(lane == line, kept_sum, 0.0) + jnp.where(lane == line + members, agree_sum, 0.0)
-    tot[me] = jnp.sum(spread, axis=0, keepdims=True)
-
-    def tot_copy(k):
-        return pltpu.make_async_remote_copy(
-            src_ref=tot.at[me], dst_ref=tot.at[me], send_sem=tot_sem.at[0], recv_sem=tot_sem.at[1],
-            device_id={"dp": lax.rem(me + k, n_dp)}, device_id_type=MESH,
-        )
-
-    tiles = tot.at[pl.ds(0, n_dp - 1)]
-    all_tot = pltpu.make_async_remote_copy(
-        src_ref=tiles, dst_ref=tiles, send_sem=tot_sem.at[0], recv_sem=tot_sem.at[1],
-        device_id={"dp": lax.rem(me + 1, n_dp)}, device_id_type=MESH,
-    )
-    for k in range(1, n_dp):
-        tot_copy(k).start()
-
-    for b in range(1, n_parts):
-        relay_part(b)
-
-    for b in range(n_parts):
-        for e in range(1, n_ens):
-            other = turn(ens, e, n_ens)
-            block_in = part.at[other, piece_of(b), :]
-            pltpu.make_async_remote_copy(
-                src_ref=block_in, dst_ref=block_in, send_sem=part_send.at[e, b], recv_sem=part_recv.at[other, b],
-                device_id={"ens": other}, device_id_type=MESH,
-            ).wait_recv()
-        total = part[0, piece_of(b), :].astype(jnp.float32)
-        for e in range(1, n_ens):
-            total += part[e, piece_of(b), :].astype(jnp.float32)
-        out_ref[piece_of(b), :] = total
-
-    all_tot.wait_recv()
-    sums = tot[0]
-    for k in range(1, n_dp):
-        sums += tot[k]
-    sums = sums / docs
-    own = members // n_ens
-    lane = lax.broadcasted_iota(jnp.int32, sums.shape, 1)
-    for j in range(own):
-        for i in range(2):
-            share_ref[i * own + j] = jnp.sum(jnp.where(lane == i * members + ens * own + j, sums, 0.0))
 
     for k in range(1, nx):
         whole = w.at[:, origin_rows(me), :]
@@ -533,6 +514,70 @@
             src_ref=blocks, dst_ref=blocks, send_sem=core_send.at[k], recv_sem=core_recv.at[0, k, 0],
             device_id={"dp": device(z, x, turn(core, k, nc))}, device_id_type=MESH,
         ).wait_send()
+    relay_part(0)
+    for k, e in others:
+        sc_arrived(k, e)
+    scores = sc_in[0]
+    for k in range(1, nx * n_ens):
+        scores += sc_in[k]
+    row = lax.broadcasted_iota(jnp.int32, (members, docs), 0)
+    cutoff = jnp.zeros((members, docs), jnp.float32)
+    mean_cutoff = jnp.float32(0.0)
+    for m in range(members):
+        level = thr[m].astype(jnp.float32) * (1.0 / 256.0)
+        cutoff = jnp.where(row == m, level, cutoff)
+        mean_cutoff += level * (1.0 / members)
+    kept = mask[...].reshape(1, docs).astype(jnp.float32) * jax.nn.sigmoid(4.0 * (scores - cutoff))
+    ens_score = jnp.sum(scores, axis=0, keepdims=True) * (1.0 / members)
+    ens_kept = jax.nn.sigmoid(4.0 * (ens_score - mean_cutoff))
+    kept_sum = jnp.sum(kept, axis=1, keepdims=True)
+    agree_sum = jnp.sum(kept * ens_kept, axis=1, keepdims=True)
+    lane = lax.broadcasted_iota(jnp.int32, (members, 128), 1)
+    line = lax.broadcasted_iota(jnp.int32, (members, 128), 0)
+    spread = jnp.where(lane == line, kept_sum, 0.0) + jnp.where(lane == line + members, agree_sum, 0.0)
+    tot[me] = jnp.sum(spread, axis=0, keepdims=True)
+
+    def tot_copy(k):
+        return pltpu.make_async_remote_copy(
+            src_ref=tot.at[me], dst_ref=tot.at[me], send_sem=tot_sem.at[0], recv_sem=tot_sem.at[1],
+            device_id={"dp": lax.rem(me + k, n_dp)}, device_id_type=MESH,
+        )
+
+    tiles = tot.at[pl.ds(0, n_dp - 1)]
+    all_tot = pltpu.make_async_remote_copy(
+        src_ref=tiles, dst_ref=tiles, send_sem=tot_sem.at[0], recv_sem=tot_sem.at[1],
+        device_id={"dp": lax.rem(me + 1, n_dp)}, device_id_type=MESH,
+    )
+    for k in range(1, n_dp):
+        tot_copy(k).start()
+
+    for b in range(1, n_parts):
+        relay_part(b)
+
+    for b in range(n_parts):
+        for e in range(1, n_ens):
+            other = turn(ens, e, n_ens)
+            block_in = part.at[other, piece_of(b), :]
+            pltpu.make_async_remote_copy(
+                src_ref=block_in, dst_ref=block_in, send_sem=part_send.at[e, b], recv_sem=part_recv.at[other, b],
+                device_id={"ens": other}, device_id_type=MESH,
+            ).wait_recv()
+        total = part[0, piece_of(b), :].astype(jnp.float32)
+        for e in range(1, n_ens):
+            total += part[e, piece_of(b), :].astype(jnp.float32)
+        out_ref[piece_of(b), :] = total
+
+    all_tot.wait_recv()
+    sums = tot[0]
+    for k in range(1, n_dp):
+        sums += tot[k]
+    sums = sums / docs
+    own = members // n_ens
+    lane = lax.broadcasted_iota(jnp.int32, sums.shape, 1)
+    for j in range(own):
+        for i in range(2):
+            share_ref[i * own + j] = jnp.sum(jnp.where(lane == i * members + ens * own + j, sums, 0.0))
+
     for k, e in others:
         sc_copy(k, e).wait_send()
     for b in range(n_parts):
@@ -575,7 +620,7 @@
                 pltpu.VMEM((members, share, classes), jnp.bfloat16),
                 pltpu.VMEM((members, nx * docs, classes), jnp.float32),
                 pltpu.VMEM((nx * docs, early * cols), jnp.bfloat16),
-                pltpu.VMEM((nx * docs, cols), jnp.float32),
+                pltpu.VMEM((chunks + nx - 1, docs, cols), jnp.float32),
                 pltpu.VMEM(valid_mask.shape, valid_mask.dtype),
                 pltpu.SMEM(thresholds.shape, thresholds.dtype),
                 pltpu.VMEM((nx, docs, classes), jnp.bfloat16),

time: 57.6 us -> 55.2 us (0.958)
  Pallas kernels: 55.5 us -> 53 us
    pallas_call x1, Pallas kernels: 55.5 us -> 53 us  [on_device(): pl.pallas_call(functools.partial(kernel, geo, n_ens), out_shape=(pltpu.VM...]
where the time goes in v3:
time: 55.2 us; the launch traced here: 55 us
  Pallas kernels  53 us (96%)
  local copies, waits for them, and re-layouts  1.35 us (2%)
  between operations  0.64 us (1%)
    pallas_call x1, Pallas kernels, on_device(): pl.pallas_call(functools.partial(kernel, geo, n_ens), out_shape=(pltpu.VM...  53 us

profile of v3, /device:TPU:0, one launch (start us, length us, event | category | flops | bytes accessed | tf_op | source)
XLA Modules:
  0.0 55.0 jit_solution(9776641122818428624)
XLA Ops:
  0.6 53.0 %shard_map.76 = (f32[768,128]{1,0:T(8,128)S(1)}, f32[2]{0:T(128)S(4)}) custom-call(bf16[768,1024]{1,0:T(8,128)(2,1)} %emb_hbm.1, s32[768]{0:T(1024)} %mask_hbm.1, bf16[2,64,2048]{2,1,0:T(8,128)(2,1)} %fw_hbm.1, bf16[2,2048,128]{2,1,0:T(8,128)(2,1)} %sw_hbm.1, s32[2]{0:T(128)} %thr_hbm.1), custom_call_target="tpu_custom_call" | custom-call | tf_op jit(solution)/shard_map/pallas_call | solution.py:609
  53.7 0.7 %copy.9 = f32[768,128]{1,0:T(8,128)} copy(f32[768,128]{1,0:T(8,128)S(1)} %get-tuple-element.9) | data formatting | bytes 786432
  54.4 0.6 %fusion = (f32[1]{0:T(128)}, f32[1]{0:T(128)}) fusion(f32[2]{0:T(128)S(4)} %get-tuple-element.6), kind=kLoop, calls=%fused_computation | loop fusion | bytes 16 | tf_op jit(solution)/shard_map/slice | solution.py:654

commit v4 on v3

--- a/solution.py
+++ b/solution.py
@@ -13,7 +13,7 @@
 ROWS = 384
 PIECES = 12
 EARLY = 1
-SPLIT = 2
+SPLIT = 3
 AHEAD = 1
 
 
@@ -198,13 +198,14 @@
 
     for k in range(1, nx):
         loop(chunks, lambda c: x_weights(k, c).start())
-        for i in range(pieces):
-            x_docs(k, i).start()
 
     def first(c):
         own_copy(c).wait()
         pass_on(c, z, x, (1, -1))
     loop(chunks, first)
+    for k in range(1, nx):
+        for i in range(pieces):
+            x_docs(k, i).start()
     for copy in (emb_copy, sw_copy, mask_copy, thr_copy):
         copy.start()
     acc[...] = jnp.zeros_like(acc)
@@ -392,13 +393,9 @@
 
     for k in range(1, nx):
         for r in range(n_blocks):
-            row = slot_block(k, r)
             far_block(chunks + k - 1, final, k, r, pl.ds(0, cols))
-            acc[final_m, row, :] += jnp.dot(
-                hid[row, 0:cols], sw[final_m, final_at, :], preferred_element_type=jnp.float32
-            )
-            if r == 0:
-                send_parts(k, range(AHEAD))
+        layer_two(final, k, pl.ds(0, cols))
+        send_parts(k, range(AHEAD))
 
     lines = -(-members // 8) * 8
     wide = members * classes
@@ -534,7 +531,11 @@
     agree_sum = jnp.sum(kept * ens_kept, axis=1, keepdims=True)
     lane = lax.broadcasted_iota(jnp.int32, (members, 128), 1)
     line = lax.broadcasted_iota(jnp.int32, (members, 128), 0)
-    spread = jnp.where(lane == line, kept_sum, 0.0) + jnp.where(lane == line + members, agree_sum, 0.0)
+    own = members // n_ens
+    mine_at = line - ens * own
+    is_mine = (mine_at >= 0) & (mine_at < own)
+    spread = jnp.where(is_mine & (lane == mine_at), kept_sum, 0.0)
+    spread += jnp.where(is_mine & (lane == mine_at + own), agree_sum, 0.0)
     tot[me] = jnp.sum(spread, axis=0, keepdims=True)
 
     def tot_copy(k):
@@ -571,12 +572,7 @@
     sums = tot[0]
     for k in range(1, n_dp):
         sums += tot[k]
-    sums = sums / docs
-    own = members // n_ens
-    lane = lax.broadcasted_iota(jnp.int32, sums.shape, 1)
-    for j in range(own):
-        for i in range(2):
-            share_ref[i * own + j] = jnp.sum(jnp.where(lane == i * members + ens * own + j, sums, 0.0))
+    share_ref[...] = sums / docs
 
     for k, e in others:
         sc_copy(k, e).wait_send()
@@ -605,15 +601,15 @@
         parts = docs // math.gcd(docs, ROWS) * SPLIT
         pieces = math.gcd(docs // n_ens // 16, PIECES)
         dma = pltpu.SemaphoreType.DMA
-        hbm, vmem, smem = (pl.BlockSpec(memory_space=s) for s in (pl.ANY, pltpu.VMEM, pltpu.SMEM))
+        hbm, vmem = (pl.BlockSpec(memory_space=s) for s in (pl.ANY, pltpu.VMEM))
         mean_logits, shares = pl.pallas_call(
             functools.partial(kernel, geo, n_ens),
             out_shape=(
                 pltpu.VMEM((docs, classes), jnp.float32),
-                pltpu.SMEM((2 * own,), jnp.float32),
+                pltpu.VMEM((1, 128), jnp.float32),
             ),
             in_specs=[hbm] * 5,
-            out_specs=(vmem, smem),
+            out_specs=(vmem, vmem),
             scratch_shapes=[
                 pltpu.VMEM((chunks, width, cols), jnp.bfloat16),
                 pltpu.VMEM((nx * docs, width), jnp.bfloat16),
@@ -651,7 +647,7 @@
                 collective_id=0, has_side_effects=True, vmem_limit_bytes=63 * 1024 * 1024
             ),
         )(embeddings, valid_mask, first_weight, second_weight, thresholds)
-        return mean_logits, shares[:own], shares[own:]
+        return mean_logits, shares[0, :own], shares[0, own : 2 * own]
 
     return jax.shard_map(
         on_device,

time: 55.2 us -> 55 us (level)
  no operation moved by 1% of the time
where the time goes in v4:
time: 55 us; the launch traced here: 54.9 us
  Pallas kernels  52.9 us (96%)
  local copies, waits for them, and re-layouts  1.33 us (2%)
  between operations  0.64 us (1%)
    pallas_call x1, Pallas kernels, on_device(): pl.pallas_call(functools.partial(kernel, geo, n_ens), out_shape=(pltpu.VM...  52.9 us

profile of v4, /device:TPU:0, one launch (start us, length us, event | category | flops | bytes accessed | tf_op | source)
XLA Modules:
  0.0 54.9 jit_solution(6403978349186023819)
XLA Ops:
  0.6 52.9 %shard_map.76 = (f32[768,128]{1,0:T(8,128)S(1)}, f32[1,128]{1,0:T(1,128)S(1)}) custom-call(bf16[768,1024]{1,0:T(8,128)(2,1)} %emb_hbm.1, s32[768]{0:T(1024)} %mask_hbm.1, bf16[2,64,2048]{2,1,0:T(8,128)(2,1)} %fw_hbm.1, bf16[2,2048,128]{2,1,0:T(8,128)(2,1)} %sw_hbm.1, s32[2]{0:T(128)} %thr_hbm.1), custom_call_target="tpu_custom_call" | custom-call | tf_op jit(solution)/shard_map/pallas_call | solution.py:605
  53.6 0.7 %copy.9 = f32[768,128]{1,0:T(8,128)} copy(f32[768,128]{1,0:T(8,128)S(1)} %get-tuple-element.9) | data formatting | bytes 786432
  54.3 0.6 %fusion = (f32[1,1]{1,0:T(1,128)}, f32[1,1]{1,0:T(1,128)}) fusion(f32[1,128]{1,0:T(1,128)S(1)} %get-tuple-element.6), kind=kLoop, calls=%fused_computation | loop fusion | bytes 16 | tf_op jit(solution)/shard_map/slice | solution.py:650
